TPU v7x, 16 devices: a whole 2x2x2 slice. The times are simulated.
16 devices in a mesh: rep: 1, dp: 16 (over x, y, z, core).
Axes of the slice: x: 2, y: 2, z: 2, core: 2. Of those that a mesh axis runs over, the one named last changes fastest.
Arguments:
- x: bfloat16 [16, 2048, 1536], P(('rep', 'dp'))
- dy: bfloat16 [16, 2048, 1536], P(('rep', 'dp'))
- w_gate: bfloat16 [2, 1536, 4224], replicated
- w_up: bfloat16 [2, 1536, 4224], replicated
- w_down: bfloat16 [2, 4224, 1536], replicated
- m_w_gate: float32 [2, 1536, 4224], P(None, 'dp')
- m_w_up: float32 [2, 1536, 4224], P(None, 'dp')
- m_w_down: float32 [2, 4224, 1536], P(None, 'dp')
- v_w_gate: float32 [2, 1536, 4224], P(None, 'dp')
- v_w_up: float32 [2, 1536, 4224], P(None, 'dp')
- v_w_down: float32 [2, 4224, 1536], P(None, 'dp')
Outputs:
- output 1: bfloat16 [2, 1536, 4224], P('rep')
- output 2: bfloat16 [2, 1536, 4224], P('rep')
- output 3: bfloat16 [2, 4224, 1536], P('rep')
- output 4: float32 [2, 1536, 4224], P('rep', 'dp')
- output 5: float32 [2, 1536, 4224], P('rep', 'dp')
- output 6: float32 [2, 4224, 1536], P('rep', 'dp')
- output 7: float32 [2, 1536, 4224], P('rep', 'dp')
- output 8: float32 [2, 1536, 4224], P('rep', 'dp')
- output 9: float32 [2, 4224, 1536], P('rep', 'dp')
All inputs are finite; a program needn't handle non-finite values.
Results may differ from a plain program's by a relative error of at most 0.022.
Values are sent between devices in bfloat16 or wider.
A program may use at most 2 GiB of HBM per device.

v0:
```python
import jax
import jax.numpy as jnp
from jax import lax

NAMES = ("w_gate", "w_up", "w_down")


def matmul(a, w):
    return jnp.dot(a, w, preferred_element_type=jnp.float32).astype(jnp.bfloat16)


def normed(h):
    wide = h.astype(jnp.float32)
    scale = lax.rsqrt(jnp.mean(wide**2, -1, keepdims=True) + 1e-6)
    return (wide * scale).astype(jnp.bfloat16)


def layer(h, w):
    a = normed(h)
    gate = jnp.dot(a, w["w_gate"], preferred_element_type=jnp.float32)
    up = jnp.dot(a, w["w_up"], preferred_element_type=jnp.float32)
    return h + matmul((jax.nn.silu(gate) * up).astype(jnp.bfloat16), w["w_down"])


def adamw(w, m, v, g):
    m = 0.9 * m + 0.1 * g
    v = 0.95 * v + 0.05 * g * g
    step = m * lax.rsqrt(v + 1e-8) + 0.1 * w
    return (w - 0.02 * step).astype(jnp.bfloat16), m, v


def clipped(gradients, sum_of_squares, count):
    factor = jnp.minimum(1.0, 0.5 * lax.rsqrt(sum_of_squares / count + 1e-30))
    return [g * factor for g in gradients]


def stack(weights, h):
    for number in range(weights["w_gate"].shape[0]):
        h = layer(h, {name: w[number] for name, w in weights.items()})
    return h


def solution(mesh):
    groups = mesh.shape["rep"]

    def step(x, dy, *arrays):
        weights, m, v = (arrays[i : i + 3] for i in (0, 3, 6))
        x, dy = (t.reshape(groups, -1, *t.shape[1:]) for t in (x, dy))

        def of_a_group(x, dy):
            _, back = jax.vjp(lambda w: stack(w, x), dict(zip(NAMES, weights, strict=True)))
            by_weights = back(dy)[0]
            gradients = [by_weights[name].astype(jnp.float32) for name in NAMES]
            gradients = clipped(gradients, sum(jnp.sum(g * g) for g in gradients), sum(g.size for g in gradients))
            new = [adamw(w.astype(jnp.float32), m, v, g) for w, m, v, g in zip(weights, m, v, gradients, strict=True)]
            return tuple(one[which] for which in range(3) for one in new)

        return tuple(t.reshape(-1, *t.shape[2:]) for t in jax.vmap(of_a_group)(x, dy))

    return step
```

profile of v0, /device:TPU:0, one launch (start us, length us, event | category | flops | bytes accessed | tf_op | source)
XLA Modules:
  0.0 3090.8 jit_solution(7149310150527470379)
XLA Ops:
  25.0 35.7 %fusion.166 = f32[2048,4224]{1,0:T(8,128)} fusion(bf16[2,1536,4224]{2,1,0:T(8,128)(2,1)} %param.12, bf16[1,2048,1536]{1,2,0:T(8,128)(2,1)S(1)} %fusion.173), kind=kOutput, calls=%fused_computation.217 | convolution fusion | flops 26575110144 | bytes 53870592 | tf_op jit(solution)/vmap(jvp())/dot_general | solution.py:20
  60.7 48.1 %fusion.150 = (bf16[1,2048,4224]{2,1,0:T(8,128)(2,1)}, f32[2048,4224]{1,0:T(8,128)}) fusion(f32[2048,4224]{1,0:T(8,128)} %fusion.166, bf16[2,1536,4224]{2,1,0:T(8,128)(2,1)} %param.17, bf16[1,2048,1536]{1,2,0:T(8,128)(2,1)} %copy-done), kind=kOutput, calls=%fused_computation.189 | convolution fusion | flops 26627014656 | bytes 105775104 | tf_op jit(solution)/vmap(jvp())/dot_general | solution.py:21
  108.7 48.7 %fusion.176 = (f32[2048]{0:T(1024)S(1)}, bf16[1,2048,1536]{1,2,0:T(8,128)(2,1)}) fusion(bf16[1,2048,1536]{1,2,0:T(8,128)(2,1)} %copy.1, bf16[2,4224,1536]{2,1,0:T(8,128)(2,1)} %param.15, bf16[1,2048,4224]{2,1,0:T(8,128)(2,1)} %get-tuple-element.263), kind=kOutput, calls=%fused_computation.227 | convolution fusion | flops 26590836736 | bytes 42868736 | tf_op jit(solution)/vmap(jvp())/dot_general | solution.py:9
  165.2 36.0 %fusion.159 = f32[2048,4224]{1,0:T(8,128)} fusion(bf16[2,1536,4224]{2,1,0:T(8,128)(2,1)} %param.17, bf16[1,2048,1536]{1,2,0:T(8,128)(2,1)S(1)} %fusion.177), kind=kOutput, calls=%fused_computation.210 | convolution fusion | flops 26575110144 | bytes 53870592 | tf_op jit(solution)/vmap(jvp())/dot_general | solution.py:21
  201.2 35.7 %convolution_convert_fusion.1 = bf16[2048,4224]{1,0:T(8,128)(2,1)} fusion(bf16[2,4224,1536]{2,1,0:T(8,128)(2,1)} %param.15, bf16[1,2048,1536]{2,1,0:T(8,128)(2,1)} %param.14), kind=kOutput, calls=%fused_computation.201 | convolution fusion | flops 26583760896 | bytes 36569088 | tf_op jit(solution)/vmap(transpose(jvp()))/dot_general | solution.py:9
  236.8 57.8 %fusion.139 = (bf16[1,2048,4224]{2,1,0:T(8,128)(2,1)}, bf16[1,2048,4224]{2,1,0:T(8,128)(2,1)}, f32[2048,4224]{1,0:T(8,128)}) fusion(f32[2048,4224]{1,0:T(8,128)} %fusion.159, bf16[2048,4224]{1,0:T(8,128)(2,1)} %convolution_convert_fusion.1, bf16[2,1536,4224]{2,1,0:T(8,128)(2,1)} %param.12, bf16[1,2048,1536]{1,2,0:T(8,128)(2,1)} %copy-done.1), kind=kOutput, calls=%fused_computation.173 | convolution fusion | flops 26704871424 | bytes 140378112 | tf_op jit(solution)/vmap(jvp())/dot_general | solution.py:20
  294.7 28.6 fusion.149
  323.3 22.8 copy.3
  346.1 333.7 %while.16 = (bf16[1,2048,4224]{1,2,0:T(8,128)(2,1)}, bf16[1,2048,1536]{2,1,0:T(8,128)(2,1)}, f32[264,1536]{1,0:T(8,128)S(1)}, f32[264,1536]{1,0:T(8,128)}, u32[]...) while((bf16[1,2048,4224]{1,2,0:T(8,128)(2,1)}, ...), condition=%wide.windowed_dot_general_cond_rs.4.clone, body=%wide.windowed_dot_general_body_rs.4.clone.sunk | while | flops 6654861312 | bytes 105579080 | solution.py:9
  375.5 33.4 %collective-permute-start.18 = (f32[264,1536]{1,0:T(8,128)}, f32[264,1536]{1,0:T(8,128)S(1)}, u32[]{:S(2)}, u32[]{:S(2)}) collective-permute-start(f32[264,1536]{1,0:T(8,128)} %get-tuple-element.491), channel_id=31, source_target_pairs={{0,1},{1,2},{2,3},{3,4},{4,5},{5,6},{6,7},{7,8},{8,9},{9,10},{10,1... | collective-permute-start | bytes 4866056 | tf_op jit(solution)/vmap(transpose(jvp()))/dot_general | solution.py:9
  473.0 18.0 collective-permute-start.18
  515.3 18.1 collective-permute-start.16
  598.8 18.4 collective-permute-start.16
  697.8 332.1 %while.14 = (bf16[1,2048,4224]{2,1,0:T(8,128)(2,1)}, bf16[1,2048,1536]{1,2,0:T(8,128)(2,1)}, f32[4224,96]{0,1:T(8,128)S(1)}, f32[4224,96]{0,1:T(8,128)}, u32[]{:...) while((bf16[1,2048,4224]{2,1,0:T(8,128)(2,1)}, ...), condition=%wide.windowed_dot_general_cond_rs.2.clone, body=%wide.windowed_dot_general_body_rs.2.clone.sunk | while | flops 6649356288 | bytes 112067192 | solution.py:21
  724.2 34.5 %collective-permute-start.10 = (f32[4224,96]{0,1:T(8,128)}, f32[4224,96]{0,1:T(8,128)S(1)}, u32[]{:S(2)}, u32[]{:S(2)}) collective-permute-start(f32[4224,96]{0,1:T(8,128)} %get-tuple-element.473), channel_id=18, source_target_pairs={{0,1},{1,2},{2,3},{3,4},{4,5},{5,6},{6,7},{7,8},{8,9},{9,10},{10,1... | collective-permute-start | bytes 4866056 | tf_op jit(solution)/vmap(transpose(jvp()))/dot_general | solution.py:21
  865.2 19.7 collective-permute-start.8
  949.2 19.5 collective-permute-start.8
  1029.9 19.7 collective-permute-start.26
  1049.6 36.0 %fusion.190 = bf16[2048,1536]{0,1:T(8,128)(2,1)} fusion(bf16[2,1536,4224]{2,1,0:T(8,128)(2,1)} %param.17, bf16[1,2048,4224]{2,1,0:T(8,128)(2,1)} %get-tuple-element.743), kind=kOutput, calls=%fused_computation.237 | convolution fusion | flops 26575110144 | bytes 36569088 | tf_op jit(solution)/vmap(transpose(jvp()))/dot_general | solution.py:21
  1094.2 38.5 %fusion.178 = (f32[2048]{0:T(1024)S(1)}, bf16[2048,1536]{0,1:T(8,128)(2,1)}) fusion(bf16[1,2048,1536]{1,2,0:T(8,128)(2,1)} %get-tuple-element.266, bf16[2048,1536]{0,1:T(8,128)(2,1)} %fusion.190, bf16[2,1536,4224]{2,1,0:T(8,128)(2,1)} %param.12, bf16[1,2048,4224]{2,1,0:T(8,128)(2,1)} %get-tuple-element.540), kind=kOutput, calls=%fused_computation.229 | convolution fusion | flops 26590836736 | bytes 49160192 | tf_op jit(solution)/vmap(transpose(jvp()))/dot_general | solution.py:20
  1144.7 56.2 %convert_multiply_fusion = (bf16[1,2048,4224]{2,1,0:T(8,128)(2,1)}, bf16[1,2048,4224]{2,1,0:T(8,128)(2,1)}) fusion(f32[2048,4224]{1,0:T(8,128)} %fusion.166, f32[2048,4224]{1,0:T(8,128)} %get-tuple-element.264, bf16[2,4224,1536]{2,1,0:T(8,128)(2,1)} %param.15, bf16[1,2048,1536]{1,2,0:T(8,128)(2,1)} %fusion.205), kind=kOutput, calls=%fused_computation.168 | convolution fusion | flops 26713522176 | bytes 123076608 | tf_op jit(solution)/vmap(transpose(jvp()))/dot_general | solution.py:9
  1200.8 329.4 %while.15 = (bf16[1,2048,4224]{2,1,0:T(8,128)(2,1)}, bf16[1,2048,1536]{1,2,0:T(8,128)(2,1)}, f32[4224,96]{0,1:T(8,128)S(1)}, f32[4224,96]{0,1:T(8,128)}, u32[]{:...) while((bf16[1,2048,4224]{2,1,0:T(8,128)(2,1)}, ...), condition=%wide.windowed_dot_general_cond_rs.3.clone, body=%wide.windowed_dot_general_body_rs.3.clone.sunk | while | flops 6649356288 | bytes 105579080 | solution.py:21
  1228.8 33.4 %collective-permute-start.14 = (f32[4224,96]{0,1:T(8,128)}, f32[4224,96]{0,1:T(8,128)S(1)}, u32[]{:S(2)}, u32[]{:S(2)}) collective-permute-start(f32[4224,96]{0,1:T(8,128)} %get-tuple-element.482), channel_id=24, source_target_pairs={{0,1},{1,2},{2,3},{3,4},{4,5},{5,6},{6,7},{7,8},{8,9},{9,10},{10,1... | collective-permute-start | bytes 4866056 | tf_op jit(solution)/vmap(transpose(jvp()))/dot_general | solution.py:21
  1367.1 18.0 collective-permute-start.12
  1407.9 18.0 collective-permute-start.14
  1450.0 18.0 collective-permute-start.12
  1490.7 18.0 collective-permute-start.14
  1530.2 18.0 collective-permute-start.27
  1556.8 22.6 copy.5
  1579.4 335.2 %while.17 = (bf16[1,2048,1536]{2,1,0:T(8,128)(2,1)}, bf16[1,2048,4224]{1,2,0:T(8,128)(2,1)}, f32[1536,264]{0,1:T(8,128)S(1)}, f32[1536,264]{0,1:T(8,128)}, u32[]...) while((bf16[1,2048,1536]{2,1,0:T(8,128)(2,1)}, ...), condition=%wide.windowed_dot_general_cond_rs.5.clone, body=%wide.windowed_dot_general_body_rs.5.clone.sunk | while | flops 6654861312 | bytes 105579080 | solution.py:9
  1607.8 33.4 %collective-permute-start.22 = (f32[1536,264]{0,1:T(8,128)}, f32[1536,264]{0,1:T(8,128)}, u32[]{:S(2)}, u32[]{:S(2)}) collective-permute-start(f32[1536,264]{0,1:T(8,128)} %get-tuple-element.500), channel_id=37, source_target_pairs={{0,1},{1,2},{2,3},{3,4},{4,5},{5,6},{6,7},{7,8},{8,9},{9,10},{10,1... | collective-permute-start | bytes 4866056 | tf_op jit(solution)/vmap(transpose(jvp()))/dot_general | solution.py:9
  1833.0 18.0 collective-permute-start.20
  1915.8 334.7 %while.12 = (bf16[1,2048,4224]{2,1,0:T(8,128)(2,1)}, bf16[1,2048,1536]{1,2,0:T(8,128)(2,1)}, f32[4224,96]{0,1:T(8,128)S(1)}, f32[4224,96]{0,1:T(8,128)}, u32[]{:...) while((bf16[1,2048,4224]{2,1,0:T(8,128)(2,1)}, ...), condition=%wide.windowed_dot_general_cond_rs.clone, body=%wide.windowed_dot_general_body_rs.clone.sunk | while | flops 6649356288 | bytes 105579080 | solution.py:20
  2001.0 18.6 collective-permute-start
  2169.2 18.0 collective-permute-start
  2250.5 334.7 %while.13 = (bf16[1,2048,4224]{2,1,0:T(8,128)(2,1)}, bf16[1,2048,1536]{1,2,0:T(8,128)(2,1)}, f32[4224,96]{0,1:T(8,128)S(1)}, f32[4224,96]{0,1:T(8,128)}, u32[]{:...) while((bf16[1,2048,4224]{2,1,0:T(8,128)(2,1)}, ...), condition=%wide.windowed_dot_general_cond_rs.1.clone, body=%wide.windowed_dot_general_body_rs.1.clone.sunk | while | flops 6649356288 | bytes 105579080 | solution.py:20
  2292.9 18.0 collective-permute-start.6
  2335.6 18.5 collective-permute-start.4
  2377.3 18.0 collective-permute-start.6
  2419.9 18.0 collective-permute-start.4
  2503.8 18.0 collective-permute-start.4
  2585.2 18.0 collective-permute-start.29
  2646.4 48.7 %all-reduce.10 = f32[]{:T(128)} all-reduce(f32[]{:T(128)S(6)} %add.180), channel_id=13, replica_groups=mesh['rep'=1,'dp'=16] {'dp'}, use_global_device_ids=true, to_apply=%region_3.4.clone | all-reduce | flops 1 | bytes 8 | tf_op jit(solution)/vmap()/reduce_sum | solution.py:54
  2715.6 94.4 %all-gather.14.cloned.1.call-done = bf16[1,2,4224,1536]{3,2,1,0:T(8,128)(2,1)} async-done(((bf16[1,2,264,1536]{3,2,1,0:T(8,128)(2,1)}), bf16[1,2,4224,1536]{3,2,1,0:T(8,128)(2,1)}) %all-gather.14.cloned.1.call-update) | async-done | bytes 25952272 | tf_op jit(solution)/reshape | solution.py:58
  2809.9 109.2 %all-gather.12.cloned.1.call-done = bf16[1,2,1536,4224]{3,2,1,0:T(8,128)(2,1)} async-done(((bf16[1,2,96,4224]{3,2,1,0:T(8,128)(2,1)}), bf16[1,2,1536,4224]{3,2,1,0:T(8,128)(2,1)}) %all-gather.12.cloned.1.call-update) | async-done | bytes 25952272 | tf_op jit(solution)/reshape | solution.py:58
  2919.2 109.2 %all-gather.10.cloned.1.call-done = bf16[1,2,1536,4224]{3,2,1,0:T(8,128)(2,1)} async-done(((bf16[1,2,96,4224]{3,2,1,0:T(8,128)(2,1)}), bf16[1,2,1536,4224]{3,2,1,0:T(8,128)(2,1)}) %all-gather.10.cloned.1.call-update) | async-done | bytes 25952272 | tf_op jit(solution)/reshape | solution.py:58
  3028.4 23.8 copy.63
  3052.3 22.6 copy.64
  (441 shorter events, 1696.1 us)
Async XLA Ops:
  7.2 2802.8 %all-gather.14.cloned.1.call-start = ((), (), s32[]{:S(2)}) async-start(), calls=%async_computation.2 | async-start | bytes 27574272 | tf_op jit(solution)/reshape | solution.py:58
  375.5 39.7 %collective-permute-start.18 = (f32[264,1536]{1,0:T(8,128)}, f32[264,1536]{1,0:T(8,128)S(1)}, u32[]{:S(2)}, u32[]{:S(2)}) collective-permute-start(f32[264,1536]{1,0:T(8,128)} %get-tuple-element.491), channel_id=31, source_target_pairs={{0,1},{1,2},{2,3},{3,4},{4,5},{5,6},{6,7},{7,8},{8,9},{9,10},{10,1... | collective-permute-start | bytes 4866056 | tf_op jit(solution)/vmap(transpose(jvp()))/dot_general | solution.py:9
  433.3 24.3 collective-permute-start.16
  473.0 24.2 collective-permute-start.18
  515.3 25.7 collective-permute-start.16
  556.4 24.2 collective-permute-start.18
  598.8 25.9 collective-permute-start.16
  679.8 1930.2 %collective-permute-start.28 = (f32[264,1536]{1,0:T(8,128)}, f32[264,1536]{1,0:T(8,128)}, u32[]{:S(2)}, u32[]{:S(2)}) collective-permute-start(f32[264,1536]{1,0:T(8,128)} %get-tuple-element.45), channel_id=32, source_target_pairs={{0,1},{1,2},{2,3},{3,4},{4,5},{5,6},{6,7},{7,8},{8,9},{9,10},{10,1... | collective-permute-start | bytes 4866056 | tf_op jit(solution)/vmap(transpose(jvp()))/dot_general | solution.py:9
  724.2 42.7 %collective-permute-start.10 = (f32[4224,96]{0,1:T(8,128)}, f32[4224,96]{0,1:T(8,128)S(1)}, u32[]{:S(2)}, u32[]{:S(2)}) collective-permute-start(f32[4224,96]{0,1:T(8,128)} %get-tuple-element.473), channel_id=18, source_target_pairs={{0,1},{1,2},{2,3},{3,4},{4,5},{5,6},{6,7},{7,8},{8,9},{9,10},{10,1... | collective-permute-start | bytes 4866056 | tf_op jit(solution)/vmap(transpose(jvp()))/dot_general | solution.py:21
  783.4 26.3 collective-permute-start.8
  823.0 25.8 collective-permute-start.10
  865.2 28.1 collective-permute-start.8
  906.5 26.2 collective-permute-start.10
  949.2 27.9 collective-permute-start.8
  990.3 25.8 collective-permute-start.10
  1029.9 1575.8 %collective-permute-start.26 = (f32[4224,96]{0,1:T(8,128)}, f32[4224,96]{0,1:T(8,128)}, u32[]{:S(2)}, u32[]{:S(2)}) collective-permute-start(f32[4224,96]{0,1:T(8,128)} %get-tuple-element.41), channel_id=19, source_target_pairs={{0,1},{1,2},{2,3},{3,4},{4,5},{5,6},{6,7},{7,8},{8,9},{9,10},{10,1... | collective-permute-start | bytes 4866056 | tf_op jit(solution)/vmap(transpose(jvp()))/dot_general | solution.py:21
  1228.8 41.6 %collective-permute-start.14 = (f32[4224,96]{0,1:T(8,128)}, f32[4224,96]{0,1:T(8,128)S(1)}, u32[]{:S(2)}, u32[]{:S(2)}) collective-permute-start(f32[4224,96]{0,1:T(8,128)} %get-tuple-element.482), channel_id=24, source_target_pairs={{0,1},{1,2},{2,3},{3,4},{4,5},{5,6},{6,7},{7,8},{8,9},{9,10},{10,1... | collective-permute-start | bytes 4866056 | tf_op jit(solution)/vmap(transpose(jvp()))/dot_general | solution.py:21
  1286.4 26.2 collective-permute-start.12
  1325.9 25.3 collective-permute-start.14
  1367.1 27.4 collective-permute-start.12
  1407.9 26.2 collective-permute-start.14
  1450.0 27.4 collective-permute-start.12
  1490.7 26.2 collective-permute-start.14
  1530.2 1077.8 %collective-permute-start.27 = (f32[4224,96]{0,1:T(8,128)}, f32[4224,96]{0,1:T(8,128)}, u32[]{:S(2)}, u32[]{:S(2)}) collective-permute-start(f32[4224,96]{0,1:T(8,128)} %get-tuple-element.43), channel_id=25, source_target_pairs={{0,1},{1,2},{2,3},{3,4},{4,5},{5,6},{6,7},{7,8},{8,9},{9,10},{10,1... | collective-permute-start | bytes 4866056 | tf_op jit(solution)/vmap(transpose(jvp()))/dot_general | solution.py:21
  1607.8 39.6 %collective-permute-start.22 = (f32[1536,264]{0,1:T(8,128)}, f32[1536,264]{0,1:T(8,128)}, u32[]{:S(2)}, u32[]{:S(2)}) collective-permute-start(f32[1536,264]{0,1:T(8,128)} %get-tuple-element.500), channel_id=37, source_target_pairs={{0,1},{1,2},{2,3},{3,4},{4,5},{5,6},{6,7},{7,8},{8,9},{9,10},{10,1... | collective-permute-start | bytes 4866056 | tf_op jit(solution)/vmap(transpose(jvp()))/dot_general | solution.py:9
  1666.0 24.3 collective-permute-start.20
  1748.8 25.5 collective-permute-start.20
  1833.0 25.6 collective-permute-start.20
  1917.2 27.4 collective-permute-start
  1958.4 26.1 collective-permute-start.2
  2001.0 28.1 collective-permute-start
  2042.9 26.1 collective-permute-start.2
  2085.5 27.4 collective-permute-start
  2126.7 26.1 collective-permute-start.2
  2169.2 27.6 collective-permute-start
  2210.6 26.1 collective-permute-start.2
  2251.8 27.4 collective-permute-start.4
  2292.9 26.2 collective-permute-start.6
  2335.6 28.0 collective-permute-start.4
  2377.3 26.2 collective-permute-start.6
  2419.9 27.4 collective-permute-start.4
  2461.2 26.2 collective-permute-start.6
  2503.8 27.4 collective-permute-start.4
  2545.0 26.2 collective-permute-start.6
  2585.2 26.8 collective-permute-start.29
  2605.7 37.0 %collective-permute-start.25 = (f32[4224,96]{0,1:T(8,128)}, f32[4224,96]{0,1:T(8,128)S(1)}, u32[]{:S(2)}, u32[]{:S(2)}) collective-permute-start(f32[4224,96]{0,1:T(8,128)} %get-tuple-element.39), channel_id=12, source_target_pairs={{0,1},{1,2},{2,3},{3,4},{4,5},{5,6},{6,7},{7,8},{8,9},{9,10},{10,1... | collective-permute-start | bytes 4866056 | tf_op jit(solution)/vmap(transpose(jvp()))/dot_general | solution.py:20
  2702.6 216.6 %all-gather.12.cloned.1.call-start = ((), (), s32[]{:S(2)}) async-start(), calls=%async_computation.1 | async-start | bytes 27574272 | tf_op jit(solution)/reshape | solution.py:58
  2709.1 319.3 %all-gather.10.cloned.1.call-start = ((), (), s32[]{:S(2)}) async-start(), calls=%async_computation | async-start | bytes 27574272 | tf_op jit(solution)/reshape | solution.py:58
  (94 other events, 2115.6 us)
Sparse Core Ops, SparseCore 0:
  2702.7 107.1 all-gather.13
  2812.8 106.3 all-gather.11
  2922.0 106.3 all-gather.9
where the time goes:
time: 3100 us; the launch traced here: 3090 us
  starting transfers between devices  944 us (30%)
  waiting for transfers between devices  860 us (28%)
  matrix products  754 us (24%)
  other arithmetic  326 us (11%)
  local copies, waits for them, and re-layouts  139 us (4%)
  blocking collectives  48.7 us (2%)
    dot_general x34, starting transfers between devices, layer(): up = jnp.dot(a, w['w_up'], preferred_element_type=jnp.float32)  329 us
    dot_general x34, starting transfers between devices, matmul(): jnp.dot(a, w, preferred_element_type=jnp.float32).astype(jnp.bfloat16)  324 us
    reshape x3, waiting for transfers between devices, step(): t.reshape(-1, *t.shape[2:])  313 us
    dot_general x34, starting transfers between devices, layer(): gate = jnp.dot(a, w['w_gate'], preferred_element_type=jnp.float32)  291 us
    dot_general x19, matrix products, layer(): gate = jnp.dot(a, w['w_gate'], preferred_element_type=jnp.float32)  263 us
    dot_general x19, matrix products, layer(): up = jnp.dot(a, w['w_up'], preferred_element_type=jnp.float32)  251 us
    dot_general x19, matrix products, matmul(): jnp.dot(a, w, preferred_element_type=jnp.float32).astype(jnp.bfloat16)  240 us
    dot_general x34, waiting for transfers between devices, matmul(): jnp.dot(a, w, preferred_element_type=jnp.float32).astype(jnp.bfloat16)  196 us
  transfers between devices with their start and end apart: 105, of which 56 were waited for; matrix products, arithmetic and copies ran while one was open for 25% of the time, Pallas kernels for 0%

commit v1 on v0

v1 whole, which is shorter than its diff:
```python
import jax
import jax.numpy as jnp
from jax import lax
from jax.sharding import PartitionSpec as P

BF, F32 = jnp.bfloat16, jnp.float32
FACTOR_COUNT = 2 * 3 * 1536 * 4224


def dot(a, b, ca, cb):
    return lax.dot_general(a, b, (((ca,), (cb,)), ((), ())), preferred_element_type=F32)


def norm(h):
    wide = h.astype(F32)
    s = lax.rsqrt(jnp.mean(wide**2, -1, keepdims=True) + 1e-6)
    return (wide * s).astype(BF), s


def norm_back(da, h, s):
    wide, da = h.astype(F32), da.astype(F32)
    return s * (da - wide * (s * s) * jnp.mean(da * wide, -1, keepdims=True))


def gates(a, wg, wu):
    return dot(a, wg, 1, 0), dot(a, wu, 1, 0)


def product(gate, up):
    return (jax.nn.silu(gate) * up).astype(BF)


def product_back(gate, up, dp):
    sig = jax.nn.sigmoid(gate)
    dp = dp.astype(F32)
    dgate = dp * up * (sig * (1 + gate * (1 - sig)))
    dup = dp * (gate * sig)
    return dgate.astype(BF), dup.astype(BF)


def adamw(w, m, v, g):
    m = 0.9 * m + 0.1 * g
    v = 0.95 * v + 0.05 * g * g
    step = m * lax.rsqrt(v + 1e-8) + 0.1 * w
    return (w - 0.02 * step).astype(BF), m, v


def solution(mesh):
    def body(x, dy, wg, wu, wd, *mv):
        x, dy = x[0], dy[0]
        rs = lambda g: lax.psum_scatter(g, "dp", scatter_dimension=0, tiled=True)
        a0, s0 = norm(x)
        gate0, up0 = gates(a0, wg[0], wu[0])
        p0 = product(gate0, up0)
        h1 = x + dot(p0, wd[0], 1, 0).astype(BF)
        a1, s1 = norm(h1)
        gate1, up1 = gates(a1, wg[1], wu[1])
        p1 = product(gate1, up1)
        gd1 = rs(dot(p1, dy, 0, 0).astype(BF))
        dp1 = dot(dy, wd[1], 1, 1).astype(BF)
        dg1, du1 = product_back(gate1, up1, dp1)
        gg1 = rs(dot(a1, dg1, 0, 0).astype(BF))
        gu1 = rs(dot(a1, du1, 0, 0).astype(BF))
        da1 = (dot(dg1, wg[1], 1, 1) + dot(du1, wu[1], 1, 1)).astype(BF)
        dh1 = (dy.astype(F32) + norm_back(da1, h1, s1)).astype(BF)
        gd0 = rs(dot(p0, dh1, 0, 0).astype(BF))
        dp0 = dot(dh1, wd[0], 1, 1).astype(BF)
        dg0, du0 = product_back(gate0, up0, dp0)
        gg0 = rs(dot(a0, dg0, 0, 0).astype(BF))
        gu0 = rs(dot(a0, du0, 0, 0).astype(BF))
        grads = [jnp.stack([gg0, gg1]), jnp.stack([gu0, gu1]), jnp.stack([gd0, gd1])]
        grads = [g.astype(F32) for g in grads]
        total = lax.psum(sum(jnp.sum(g * g) for g in grads), "dp")
        factor = jnp.minimum(1.0, 0.5 * lax.rsqrt(total / FACTOR_COUNT + 1e-30))
        me = lax.axis_index("dp")
        ws = []
        for w in (wg, wu, wd):
            rows = w.shape[1] // 16
            ws.append(lax.dynamic_slice_in_dim(w, me * rows, rows, 1))
        new = [adamw(w.astype(F32), m, v, g * factor) for w, m, v, g in zip(ws, mv[:3], mv[3:], grads)]
        full = [lax.all_gather(n[0], "dp", axis=1, tiled=True) for n in new]
        return (*full, *(n[1] for n in new), *(n[2] for n in new))

    seq, whole, block = P(("rep", "dp"), None, None), P(None, None, None), P(None, "dp", None)
    out_whole, out_block = P("rep", None, None), P("rep", "dp", None)
    return jax.shard_map(
        body, mesh=mesh,
        in_specs=(seq, seq, whole, whole, whole, *(block,) * 6),
        out_specs=(out_whole,) * 3 + (out_block,) * 6,
        check_vma=False,
    )
```

time: 3100 us -> 1430 us (0.46)
  starting transfers between devices: 944 us -> 0.37 us
  other arithmetic: 326 us -> 40.1 us
  waiting for transfers between devices: 860 us -> 658 us
  matrix products: 754 us -> 598 us
  local copies, waits for them, and re-layouts: 139 us -> 73.7 us
    dot_general x102 -> x0, starting transfers between devices: 944 us -> none  [the longest x34 329 us: layer(): up = jnp.dot(a, w['w_up'], preferred_element_type=jnp.float32)]
    dot_general x102 -> x0, waiting for transfers between devices: 547 us -> none  [the longest x34 196 us: matmul(): jnp.dot(a, w, preferred_element_type=jnp.float32).astype(jnp.bfloat16)]
    reduce_scatter x0 -> x6, waiting for transfers between devices: none -> 345 us  [body(): rs = lambda g: lax.psum_scatter(g, 'dp', scatter_dimension=0, tiled=True)]
    reshape x3 -> x0, waiting for transfers between devices: 313 us -> none  [step(): t.reshape(-1, *t.shape[2:])]
    all_gather x0 -> x3, waiting for transfers between devices: none -> 313 us  [body(): full = [lax.all_gather(n[0], 'dp', axis=1, tiled=True) for n in new]]
    dot_general x96 -> x0, other arithmetic: 242 us -> none
    dot_general x57 -> x15, matrix products: 754 us -> 598 us  [dot(): lax.dot_general(a, b, (((ca,), (cb,)), ((), ())), preferred_element_type=...]
    unnamed x74 -> x43, local copies, waits for them, and re-layouts: 134 us -> 73.7 us
  transfers between devices with their start and end apart: 105 -> 9, of which waited for: 56 -> 7; matrix products, arithmetic and copies ran while one was open for 25% -> 18% of each run, Pallas kernels for 0% -> 0%
where the time goes in v1:
time: 1430 us; the launch traced here: 1420 us
  waiting for transfers between devices  658 us (46%)
  matrix products  598 us (42%)
  local copies, waits for them, and re-layouts  73.7 us (5%)
  other arithmetic  40.1 us (3%)
  blocking collectives  31.8 us (2%)
  between operations  17.1 us (1%)
    dot_general x15, matrix products, dot(): lax.dot_general(a, b, (((ca,), (cb,)), ((), ())), preferred_element_type=...  598 us
    reduce_scatter x6, waiting for transfers between devices, body(): rs = lambda g: lax.psum_scatter(g, 'dp', scatter_dimension=0, tiled=True)  345 us
    all_gather x3, waiting for transfers between devices, body(): full = [lax.all_gather(n[0], 'dp', axis=1, tiled=True) for n in new]  313 us
    unnamed x43, local copies, waits for them, and re-layouts  73.7 us
    psum x1, blocking collectives, body(): total = lax.psum(sum((jnp.sum(g * g) for g in grads)), 'dp')  31.8 us
  transfers between devices with their start and end apart: 9, of which 7 were waited for; matrix products, arithmetic and copies ran while one was open for 18% of the time, Pallas kernels for 0%

profile of v1, /device:TPU:0, one launch (start us, length us, event | category | flops | bytes accessed | tf_op | source)
XLA Modules:
  0.0 1419.1 jit_solution(5933425903061891676)
XLA Ops:
  7.2 0.0 reduce-scatter.15.cloned.1.call-start
  7.2 8.7 copy.20
  15.9 4.1 fusion.29
  20.0 37.5 %fusion.24 = f32[2048,4224]{1,0:T(8,128)} fusion(bf16[2,1536,4224]{2,1,0:T(8,128)(2,1)} %param.13, bf16[1,2048,1536]{2,1,0:T(8,128)(2,1)} %param.11, f32[2048]{0:T(1024)S(1)} %add_rsqrt_fusion.1), kind=kOutput, calls=%fused_computation.45 | convolution fusion | flops 26584547328 | bytes 53878784 | tf_op jit(solution)/shard_map/dot_general | solution.py:11
  57.5 42.6 %multiply_convert_fusion.1 = (bf16[2048,4224]{1,0:T(8,128)(2,1)}, f32[2048,4224]{1,0:T(8,128)}) fusion(f32[2048,4224]{1,0:T(8,128)} %fusion.24, bf16[2,1536,4224]{2,1,0:T(8,128)(2,1)} %param.14, bf16[1,2048,1536]{2,1,0:T(8,128)(2,1)} %param.11, f32[2048]{0:T(1024)S(1)} %add_rsqrt_fusion.1), kind=kOutput, calls=%fused_computation.13 | convolution fusion | flops 26636451840 | bytes 105783296 | tf_op jit(solution)/shard_map/dot_general | solution.py:11
  100.2 48.7 %fusion.34 = (f32[2048]{0:T(1024)S(1)}, bf16[2048,1536]{0,1:T(8,128)(2,1)}) fusion(bf16[2048,4224]{1,0:T(8,128)(2,1)} %get-tuple-element.22, bf16[2,4224,1536]{2,1,0:T(8,128)(2,1)} %param.15, bf16[1,2048,1536]{1,2,0:T(8,128)(2,1)} %copy.20), kind=kOutput, calls=%fused_computation.55 | convolution fusion | flops 26590836736 | bytes 42868736 | tf_op jit(solution)/shard_map/dot_general | solution.py:11
  148.9 0.6 fusion.88
  149.5 37.4 %fusion.16 = f32[2048,4224]{1,0:T(8,128)} fusion(bf16[2,1536,4224]{2,1,0:T(8,128)(2,1)} %param.14, bf16[2048,1536]{0,1:T(8,128)(2,1)} %get-tuple-element.25, f32[2048]{0:T(1024)S(1)} %get-tuple-element.21), kind=kOutput, calls=%fused_computation.37 | convolution fusion | flops 26584547328 | bytes 53878784 | tf_op jit(solution)/shard_map/dot_general | solution.py:11
  186.9 36.0 %fusion.12 = f32[2048,4224]{1,0:T(8,128)} fusion(bf16[2,1536,4224]{2,1,0:T(8,128)(2,1)} %param.13, bf16[2048,1536]{0,1:T(8,128)(2,1)S(1)} %copy-done, f32[2048]{0:T(1024)S(1)} %get-tuple-element.21), kind=kOutput, calls=%fused_computation.33 | convolution fusion | flops 26584547328 | bytes 53878784 | tf_op jit(solution)/shard_map/dot_general | solution.py:11
  222.9 8.7 copy.21
  231.6 52.3 %fusion.2 = (bf16[2048,4224]{1,0:T(8,128)(2,1)}, bf16[2048,4224]{1,0:T(8,128)(2,1)}) fusion(f32[2048,4224]{1,0:T(8,128)} %fusion.12, f32[2048,4224]{1,0:T(8,128)} %fusion.16, bf16[2,4224,1536]{2,1,0:T(8,128)(2,1)} %param.15, bf16[1,2048,1536]{2,1,0:T(8,128)(2,1)} %param.12), kind=kOutput, calls=%fused_computation.6 | convolution fusion | flops 26704871424 | bytes 123076608 | tf_op jit(solution)/shard_map/dot_general | solution.py:11
  283.9 36.6 %fusion.10 = f32[2048,1536]{0,1:T(8,128)} fusion(bf16[2048,4224]{1,0:T(8,128)(2,1)} %get-tuple-element.19, bf16[2,1536,4224]{2,1,0:T(8,128)(2,1)} %param.13), kind=kOutput, calls=%fused_computation.31 | convolution fusion | flops 26575110144 | bytes 42860544 | tf_op jit(solution)/shard_map/dot_general | solution.py:11
  320.5 38.1 %fusion.37 = (f32[2048]{0:T(1024)S(1)}, bf16[2048,1536]{0,1:T(8,128)(2,1)}) fusion(bf16[2048,1536]{0,1:T(8,128)(2,1)} %get-tuple-element.25, f32[2048,1536]{0,1:T(8,128)} %fusion.10, bf16[2048,4224]{1,0:T(8,128)(2,1)} %get-tuple-element.18, bf16[2,1536,4224]{2,1,0:T(8,128)(2,1)} %param.14), kind=kOutput, calls=%fused_computation.58 | convolution fusion | flops 26593982464 | bytes 55451648 | tf_op jit(solution)/shard_map/dot_general | solution.py:11
  358.6 8.1 fusion.33
  366.8 34.3 %convolution_convert_fusion.7 = bf16[4224,1536]{1,0:T(8,128)(2,1)} fusion(bf16[2048,4224]{1,0:T(8,128)(2,1)} %get-tuple-element.22, bf16[2048,1536]{0,1:T(8,128)(2,1)} %fusion.33), kind=kOutput, calls=%fused_computation.27 | convolution fusion | flops 26581598208 | bytes 36569088 | tf_op jit(solution)/shard_map/dot_general | solution.py:11
  401.1 0.0 reduce-scatter.17.cloned.1.call-start
  401.2 39.5 %convolution_convert_fusion.6 = bf16[4224,1536]{1,0:T(8,128)(2,1)} fusion(f32[2048,4224]{1,0:T(8,128)} %fusion.16, bf16[1,2048,1536]{2,1,0:T(8,128)(2,1)} %param.12, f32[2048,4224]{1,0:T(8,128)} %fusion.12), kind=kOutput, calls=%fused_computation.26 | convolution fusion | flops 26633502720 | bytes 88473600 | tf_op jit(solution)/shard_map/dot_general | solution.py:11
  440.7 0.0 reduce-scatter.11.cloned.1.call-start
  440.8 36.2 %convolution_convert_fusion.4 = bf16[2048,4224]{1,0:T(8,128)(2,1)} fusion(bf16[2048,1536]{0,1:T(8,128)(2,1)} %fusion.33, bf16[2,4224,1536]{2,1,0:T(8,128)(2,1)} %param.15), kind=kOutput, calls=%fused_computation.24 | convolution fusion | flops 26583760896 | bytes 36569088 | tf_op jit(solution)/shard_map/dot_general | solution.py:11
  477.0 43.1 %convolution_convert_fusion.1 = bf16[1536,4224]{1,0:T(8,128)(2,1)} fusion(bf16[2048,4224]{1,0:T(8,128)(2,1)} %convolution_convert_fusion.4, f32[2048,4224]{1,0:T(8,128)} %fusion.24, bf16[1,2048,1536]{1,2,0:T(8,128)(2,1)} %copy.20, f32[2048]{0:T(1024)S(1)} %copy-done.9), kind=kOutput, calls=%fused_computation.21 | convolution fusion | flops 26651590656 | bytes 71180288 | tf_op jit(solution)/shard_map/dot_general | solution.py:11
  520.1 0.0 reduce-scatter.13.cloned.1.call-start
  520.1 0.6 copy-done.6
  520.8 35.7 %convolution_convert_fusion = bf16[1536,4224]{1,0:T(8,128)(2,1)} fusion(bf16[2048,4224]{1,0:T(8,128)(2,1)} %get-tuple-element.18, bf16[2048,1536]{0,1:T(8,128)(2,1)} %get-tuple-element.25, f32[2048]{0:T(1024)S(1)} %copy-done.6), kind=kOutput, calls=%fused_computation.20 | convolution fusion | flops 26591035392 | bytes 36577280 | tf_op jit(solution)/shard_map/dot_general | solution.py:11
  556.5 0.0 reduce-scatter.7.cloned.1.call-start
  556.5 44.3 %convolution_convert_fusion.3 = bf16[1536,4224]{1,0:T(8,128)(2,1)} fusion(f32[2048,4224]{1,0:T(8,128)} %get-tuple-element.23, bf16[2048,4224]{1,0:T(8,128)(2,1)} %convolution_convert_fusion.4, f32[2048,4224]{1,0:T(8,128)} %fusion.24, bf16[1,2048,1536]{1,2,0:T(8,128)(2,1)} %copy.20, f32[2048]{0:T(1024)S(1)} %copy-done.9), kind=kOutput, calls=%fused_computation.23 | convolution fusion | flops 26686193664 | bytes 105783296 | tf_op jit(solution)/shard_map/dot_general | solution.py:11
  600.8 0.0 reduce-scatter.9.cloned.1.call-start
  600.9 35.7 %convolution_convert_fusion.2 = bf16[1536,4224]{1,0:T(8,128)(2,1)} fusion(bf16[2048,4224]{1,0:T(8,128)(2,1)} %get-tuple-element.19, bf16[2048,1536]{0,1:T(8,128)(2,1)} %get-tuple-element.25, f32[2048]{0:T(1024)S(1)} %copy-done.6), kind=kOutput, calls=%fused_computation.22 | convolution fusion | flops 26591035392 | bytes 36577280 | tf_op jit(solution)/shard_map/dot_general | solution.py:11
  636.6 0.0 all-gather.8.cloned.1.call-start
  636.6 0.0 reduce-scatter.15.cloned.1.call-done
  636.7 3.0 fusion.73
  639.7 53.4 %reduce-scatter.11.cloned.1.call-done = bf16[96,4224]{1,0:T(8,128)(2,1)} async-done(((bf16[1536,4224]{1,0:T(8,128)(2,1)}), bf16[96,4224]{1,0:T(8,128)(2,1)}) %reduce-scatter.11.cloned.1.call-update) | async-done | bytes 811024 | tf_op jit(solution)/shard_map/reduce_scatter | solution.py:51
  693.1 97.8 %reduce-scatter.13.cloned.1.call-done = bf16[96,4224]{1,0:T(8,128)(2,1)} async-done(((bf16[1536,4224]{1,0:T(8,128)(2,1)}), bf16[96,4224]{1,0:T(8,128)(2,1)}) %reduce-scatter.13.cloned.1.call-update) | async-done | bytes 811024 | tf_op jit(solution)/shard_map/reduce_scatter | solution.py:51
  790.9 2.8 fusion.72
  793.7 95.5 %reduce-scatter.7.cloned.1.call-done = bf16[96,4224]{1,0:T(8,128)(2,1)} async-done(((bf16[1536,4224]{1,0:T(8,128)(2,1)}), bf16[96,4224]{1,0:T(8,128)(2,1)}) %reduce-scatter.7.cloned.1.call-update) | async-done | bytes 811024 | tf_op jit(solution)/shard_map/reduce_scatter | solution.py:51
  889.2 98.4 %reduce-scatter.9.cloned.1.call-done = bf16[96,4224]{1,0:T(8,128)(2,1)} async-done(((bf16[1536,4224]{1,0:T(8,128)(2,1)}), bf16[96,4224]{1,0:T(8,128)(2,1)}) %reduce-scatter.9.cloned.1.call-update) | async-done | bytes 811024 | tf_op jit(solution)/shard_map/reduce_scatter | solution.py:51
  987.6 2.8 fusion.71
  992.4 31.8 %psum.7 = f32[]{:T(128)} all-reduce(f32[]{:T(128)S(6)} %add.123), channel_id=1, replica_groups=mesh['rep'=1,'dp'=16] {'dp'}, use_global_device_ids=true, to_apply=%region_12.13 | all-reduce | flops 1 | bytes 8 | tf_op jit(solution)/shard_map/psum | solution.py:73
  1024.9 5.7 fusion.79
  1030.6 0.0 all-gather.6.cloned.1.call-start
  1030.7 6.8 fusion.76
  1037.5 0.0 all-gather.4.cloned.1.call-start
  1037.6 6.1 fusion.70
  1043.7 94.3 %all-gather.8.cloned.1.call-done = bf16[2,4224,1536]{2,1,0:T(8,128)(2,1)} async-done(((bf16[2,264,1536]{2,1,0:T(8,128)(2,1)}), bf16[2,4224,1536]{2,1,0:T(8,128)(2,1)}) %all-gather.8.cloned.1.call-update) | async-done | bytes 25952272 | tf_op jit(solution)/shard_map/all_gather | solution.py:81
  1138.0 109.2 %all-gather.6.cloned.1.call-done = bf16[2,1536,4224]{2,1,0:T(8,128)(2,1)} async-done(((bf16[2,96,4224]{2,1,0:T(8,128)(2,1)}), bf16[2,1536,4224]{2,1,0:T(8,128)(2,1)}) %all-gather.6.cloned.1.call-update) | async-done | bytes 25952272 | tf_op jit(solution)/shard_map/all_gather | solution.py:81
  1247.2 109.2 %all-gather.4.cloned.1.call-done = bf16[2,1536,4224]{2,1,0:T(8,128)(2,1)} async-done(((bf16[2,96,4224]{2,1,0:T(8,128)(2,1)}), bf16[2,1536,4224]{2,1,0:T(8,128)(2,1)}) %all-gather.4.cloned.1.call-update) | async-done | bytes 25952272 | tf_op jit(solution)/shard_map/all_gather | solution.py:81
  1356.4 23.8 %copy.25 = bf16[2,1536,4224]{2,1,0:T(8,128)(2,1)} copy(bf16[2,1536,4224]{2,1,0:T(8,128)(2,1)} %all-gather.4.cloned.1.call-done) | data formatting | bytes 51904512
  1380.3 22.6 %copy.26 = bf16[2,1536,4224]{2,1,0:T(8,128)(2,1)} copy(bf16[2,1536,4224]{2,1,0:T(8,128)(2,1)} %all-gather.6.cloned.1.call-done) | data formatting | bytes 51904512
  1402.9 9.2 copy.27
  (51 shorter events, 0.3 us)
Async XLA Ops:
  7.2 629.5 %reduce-scatter.15.cloned.1.call-start = ((), (), s32[]{:S(2)}) async-start(), calls=%async_computation.10 | async-start | bytes 13787136 | tf_op jit(solution)/shard_map/reduce_scatter | solution.py:51
  20.0 37.5 %copy-start.8 = (f32[2048]{0:T(1024)}, f32[2048]{0:T(1024)S(1)}, u32[]{:S(2)}) copy-start(f32[2048]{0:T(1024)S(1)} %add_rsqrt_fusion.1) | copy-start | bytes 24580
  149.5 37.4 %copy-start.4 = (f32[2048]{0:T(1024)}, f32[2048]{0:T(1024)S(1)}, u32[]{:S(2)}) copy-start(f32[2048]{0:T(1024)S(1)} %get-tuple-element.21) | copy-start | bytes 24580
  149.5 37.4 %copy-start = (bf16[2048,1536]{0,1:T(8,128)(2,1)S(1)}, bf16[2048,1536]{0,1:T(8,128)(2,1)}, u32[]{:S(2)}) copy-start(bf16[2048,1536]{0,1:T(8,128)(2,1)} %get-tuple-element.25) | copy-start | bytes 18874372
  283.9 74.7 %slice-start.7 = ((s8[6291456]{0:T(1024)(128)(4,1)}), s8[2097152]{0:T(1024)(128)(4,1)S(1)}, s32[]{:S(2)}) async-start(s8[6291456]{0:T(1024)(128)(4,1)} %bitcast.82), calls=%async_computation.22 | async-start | bytes 4194304
  320.5 38.1 %slice-start.8 = ((s8[6291456]{0:T(1024)(128)(4,1)}), s8[4194304]{0:T(1024)(128)(4,1)S(1)}, s32[]{:S(2)}) async-start(s8[6291456]{0:T(1024)(128)(4,1)} %bitcast.82), calls=%async_computation.23 | async-start | bytes 8388608
  320.5 38.1 %copy-start.1 = (bf16[2048,1536]{0,1:T(8,128)(2,1)S(1)}, bf16[2048,1536]{0,1:T(8,128)(2,1)}, u32[]{:S(2)}) copy-start(bf16[2048,1536]{0,1:T(8,128)(2,1)} %get-tuple-element.25) | copy-start | bytes 18874372
  320.5 38.1 %copy-start.5 = (f32[2048]{0:T(1024)S(1)}, f32[2048]{0:T(1024)}, u32[]{:S(2)}) copy-start(f32[2048]{0:T(1024)} %copy-done.4) | copy-start | bytes 24580
  320.5 38.1 %copy-start.7 = (f32[2048]{0:T(1024)S(1)}, f32[2048]{0:T(1024)}, u32[]{:S(2)}) copy-start(f32[2048]{0:T(1024)} %get-tuple-element.20) | copy-start | bytes 24580
  401.1 235.6 %reduce-scatter.17.cloned.1.call-start = ((), (), s32[]{:S(2)}) async-start(), calls=%async_computation.11 | async-start | bytes 13787136 | tf_op jit(solution)/shard_map/reduce_scatter | solution.py:51
  440.7 36.3 %copy-start.9 = (f32[2048]{0:T(1024)S(1)}, f32[2048]{0:T(1024)}, u32[]{:S(2)}) copy-start(f32[2048]{0:T(1024)} %copy-done.8) | copy-start | bytes 24580
  440.7 252.4 %reduce-scatter.11.cloned.1.call-start = ((), (), s32[]{:S(2)}) async-start(), calls=%async_computation.8 | async-start | bytes 13787136 | tf_op jit(solution)/shard_map/reduce_scatter | solution.py:51
  520.1 0.7 copy-start.6
  520.1 270.8 %reduce-scatter.13.cloned.1.call-start = ((), (), s32[]{:S(2)}) async-start(), calls=%async_computation.9 | async-start | bytes 13787136 | tf_op jit(solution)/shard_map/reduce_scatter | solution.py:51
  556.5 332.8 %reduce-scatter.7.cloned.1.call-start = ((), (), s32[]{:S(2)}) async-start(), calls=%async_computation.6 | async-start | bytes 13787136 | tf_op jit(solution)/shard_map/reduce_scatter | solution.py:51
  600.8 386.8 %reduce-scatter.9.cloned.1.call-start = ((), (), s32[]{:S(2)}) async-start(), calls=%async_computation.7 | async-start | bytes 13787136 | tf_op jit(solution)/shard_map/reduce_scatter | solution.py:51
  636.6 388.4 %copy-start.2 = (f32[2,264,1536]{2,1,0:T(8,128)S(1)}, f32[2,264,1536]{2,1,0:T(8,128)}, u32[]{:S(2)}) copy-start(f32[2,264,1536]{2,1,0:T(8,128)} %param.21) | copy-start | bytes 9732100
  636.6 501.4 %all-gather.8.cloned.1.call-start = ((), (), s32[]{:S(2)}) async-start(), calls=%async_computation.14 | async-start | bytes 27574272 | tf_op jit(solution)/shard_map/all_gather | solution.py:81
  1030.6 7.0 copy-start.3
  1030.6 216.6 %all-gather.6.cloned.1.call-start = ((), (), s32[]{:S(2)}) async-start(), calls=%async_computation.13 | async-start | bytes 27574272 | tf_op jit(solution)/shard_map/all_gather | solution.py:81
  1037.5 318.9 %all-gather.4.cloned.1.call-start = ((), (), s32[]{:S(2)}) async-start(), calls=%async_computation.12 | async-start | bytes 27574272 | tf_op jit(solution)/shard_map/all_gather | solution.py:81
  1356.4 46.4 %slice-start = ((s8[25952256]{0:T(1024)(128)(4,1)}), s8[4194304]{0:T(1024)(128)(4,1)S(1)}, s32[]{:S(2)}) async-start(s8[25952256]{0:T(1024)(128)(4,1)} %bitcast.80), calls=%async_computation.15 | async-start | bytes 8388608
  1356.4 46.4 %slice-start.1 = ((s8[25952256]{0:T(1024)(128)(4,1)}), s8[4194304]{0:T(1024)(128)(4,1)S(1)}, s32[]{:S(2)}) async-start(s8[25952256]{0:T(1024)(128)(4,1)} %bitcast.80), calls=%async_computation.16 | async-start | bytes 8388608
  1356.4 46.4 %slice-start.2 = ((s8[25952256]{0:T(1024)(128)(4,1)}), s8[4194304]{0:T(1024)(128)(4,1)S(1)}, s32[]{:S(2)}) async-start(s8[25952256]{0:T(1024)(128)(4,1)} %bitcast.80), calls=%async_computation.17 | async-start | bytes 8388608
  1356.4 46.4 %slice-start.3 = ((s8[25952256]{0:T(1024)(128)(4,1)}), s8[4194304]{0:T(1024)(128)(4,1)S(1)}, s32[]{:S(2)}) async-start(s8[25952256]{0:T(1024)(128)(4,1)} %bitcast.80), calls=%async_computation.18 | async-start | bytes 8388608
  1380.3 22.6 %slice-start.4 = ((s8[25952256]{0:T(1024)(128)(4,1)}), s8[4194304]{0:T(1024)(128)(4,1)S(1)}, s32[]{:S(2)}) async-start(s8[25952256]{0:T(1024)(128)(4,1)} %bitcast.80), calls=%async_computation.19 | async-start | bytes 8388608
  1380.3 22.6 %slice-start.5 = ((s8[25952256]{0:T(1024)(128)(4,1)}), s8[4194304]{0:T(1024)(128)(4,1)S(1)}, s32[]{:S(2)}) async-start(s8[25952256]{0:T(1024)(128)(4,1)} %bitcast.80), calls=%async_computation.20 | async-start | bytes 8388608
  1380.3 22.6 %slice-start.6 = ((s8[25952256]{0:T(1024)(128)(4,1)}), s8[786432]{0:T(1024)(128)(4,1)S(1)}, s32[]{:S(2)}) async-start(s8[25952256]{0:T(1024)(128)(4,1)} %bitcast.80), calls=%async_computation.21 | async-start | bytes 1572864
Sparse Core Ops, SparseCore 0:
  401.3 95.9 reduce-scatter.14
  502.0 93.1 reduce-scatter.16
  599.9 93.1 reduce-scatter.10
  697.7 93.1 reduce-scatter.12
  796.1 93.1 reduce-scatter.6
  894.5 93.1 reduce-scatter.8
  1030.7 107.1 all-gather.7
  1140.8 106.3 all-gather.5
  1250.0 106.3 all-gather.3
